TPU v7x, 32 devices: a whole 2x2x4 slice. The times are simulated.
32 devices in a mesh: aux: 8 (over z, x), lmo: 4 (over y, core).
Axes of the slice: x: 2, y: 2, z: 4, core: 2. Of those that a mesh axis runs over, the one named last changes fastest.
Arguments:
- aux_ints: bfloat16 [256, 768, 768], P(('aux', 'lmo')), may hold values from -6 to 6
- lmo_coef: bfloat16 [128, 384], P(('aux', 'lmo')), may hold values from -0.3125 to 0.3125
- ao_domain: int32 [128, 3], replicated, may hold values from 0 to 5, as said below
- ao_count: int32 [128], replicated, may hold values from 1 to 3
- pao_domain: int32 [128, 3], replicated, may hold values from 0 to 5, as said below
- pao_count: int32 [128], replicated, may hold values from 1 to 3, as said below
- owner_order: int32 [128], replicated, may hold values from 0 to 127, as said below
- pao_coef: bfloat16 [128, 384, 256], P(('aux', 'lmo')), may hold values from -0.3125 to 0.3125
Outputs:
- pair_ints: bfloat16 [128, 256, 256], P(('aux', 'lmo'))
- pair_metric: float32 [128, 256, 256], P(('aux', 'lmo'))
Inputs may be any that keep to these rules, and one draw needn't show every extreme that they name: `ao_domain`: each row holds 3 different block numbers; slots from ao_count on are unused. `pao_domain`: each row holds 3 different block numbers; slots from pao_count on are unused. `pao_count`: the LMOs of the 4 owner slots of one device use together at most 8 PAO block slots, and those of some device use exactly 8. `owner_order`: every LMO stands in exactly one slot.
All inputs are finite; a program needn't handle non-finite values.
Results may differ from a plain program's by a relative error of at most 0.0049.
Values may be sent and summed in bfloat16 or wider, within the bound.
A program may use at most 128 MiB of HBM per device.

v0:
```python
import jax
import jax.numpy as jnp
from jax import lax
from jax.sharding import PartitionSpec as P

BLK = 128
DB = 3
PB = 3


def place(lmo_coef, domain, block_count, blocks):
    lmo_total = lmo_coef.shape[0]
    in_domain = jnp.arange(DB)[None, :] < block_count[:, None]
    onehot = (
        (domain[:, :, None] == jnp.arange(blocks)[None, None, :]) & in_domain[:, :, None]
    ).astype(jnp.float32)
    tiles = lmo_coef.astype(jnp.float32).reshape(lmo_total, DB, BLK)
    dense_coef = jnp.einsum("ikb,ikn->bni", onehot, tiles, precision=lax.Precision.HIGHEST)
    return dense_coef.reshape(blocks * BLK, lmo_total).astype(jnp.bfloat16)


def select(half_ints, domain, block_count, blocks):
    row_total = half_ints.shape[0]
    lmo_total = half_ints.shape[2]
    in_domain = jnp.arange(PB)[None, :] < block_count[:, None]
    onehot = (
        (domain[:, :, None] == jnp.arange(blocks)[None, None, :]) & in_domain[:, :, None]
    ).astype(jnp.float32)
    tiled = half_ints.reshape(row_total, blocks, BLK, lmo_total)
    picked = jnp.einsum("pbni,ikb->ipkn", tiled, onehot, precision=lax.Precision.HIGHEST)
    return picked.reshape(lmo_total, row_total, PB * BLK).astype(jnp.bfloat16)


def shards(aux_ints, lmo_coef, ao_domain, ao_count, pao_domain, pao_count, owner_order, pao_coef):
    all_coef = lax.all_gather(lmo_coef, ("aux", "lmo"), axis=0, tiled=True)
    row_total, ao_total, _ = aux_ints.shape
    blocks = ao_total // BLK
    dense_coef = place(all_coef, ao_domain, ao_count, blocks)
    half_ints = jnp.dot(
        aux_ints.reshape(row_total * ao_total, ao_total),
        dense_coef,
        preferred_element_type=jnp.float32,
    ).reshape(row_total, ao_total, -1)
    selected = select(half_ints, pao_domain, pao_count, blocks)
    ordered = jnp.take(selected, owner_order, axis=0)
    received = lax.all_to_all(ordered, ("aux", "lmo"), split_axis=0, concat_axis=1, tiled=True)
    aux_total = received.shape[1]
    pair_ints = jnp.einsum(
        "rpm,rma->rpa", received, pao_coef, preferred_element_type=jnp.float32
    ).astype(jnp.bfloat16)
    pair_metric = (
        jnp.einsum("rpa,rpb->rab", pair_ints, pair_ints, preferred_element_type=jnp.float32)
        / aux_total
    )
    return (pair_ints, pair_metric)


def solution(mesh):
    placed = (
        P(("aux", "lmo"), None, None),
        P(("aux", "lmo"), None),
        P(),
        P(),
        P(),
        P(),
        P(),
        P(("aux", "lmo"), None, None),
    )
    return jax.shard_map(
        shards,
        mesh=mesh,
        in_specs=placed,
        out_specs=(P(("aux", "lmo"), None, None), P(("aux", "lmo"), None, None)),
        check_vma=False,
    )
```

profile of v0, /device:TPU:0, one launch (start us, length us, event | category | flops | bytes accessed | tf_op | source)
XLA Modules:
  0.0 96.0 jit_solution(15737107026913845663)
XLA Ops:
  0.6 0.0 copy-start
  0.6 0.7 compare_select_fusion
  1.4 0.7 compare_and_fusion
  2.0 43.7 %all-gather = bf16[32,4,384]{2,1,0:T(4,128)(2,1)S(1)} all-gather(bf16[1,4,384]{2,1,0:T(4,128)(2,1)} %bitcast.32), channel_id=1, replica_groups=mesh['aux'=8,'lmo'=4] {'aux','lmo'}, dimensions={0}, use_global_device_ids=true | all-gather | bytes 101376 | tf_op jit(solution)/shard_map/all_gather | solution.py:35
  45.8 0.8 copy.22
  46.6 0.7 iota_compare_fusion.2
  47.4 0.9 fusion.1
  48.3 0.2 copy.23
  48.5 8.5 %convolution_bitcast_fusion = f32[6144,128]{0,1:T(8,128)} fusion(bf16[768,128]{1,0:T(8,128)(2,1)S(1)} %bitcast.30, bf16[6144,768]{1,0:T(8,128)(2,1)} %bitcast.28), kind=kOutput, calls=%fused_computation.1 | convolution fusion | flops 1207959552 | bytes 12779520 | tf_op jit(solution)/shard_map/dot_general | solution.py:39
  57.0 3.6 %copy.24 = f32[6144,128]{1,0:T(8,128)} copy(f32[6144,128]{0,1:T(8,128)} %convolution_bitcast_fusion) | data formatting | bytes 6291456 | tf_op jit(solution)/shard_map/dot_general | solution.py:39
  60.6 0.0 copy-start.2
  60.6 0.0 copy-start.3
  60.6 5.0 %copy.25 = f32[8,6,128,128]{2,1,0,3:T(8,128)} copy(f32[8,6,128,128]{3,2,1,0:T(8,128)} %bitcast.29) | data formatting | bytes 6291456 | tf_op jit(solution)/shard_map/reshape;reshape | solution.py:29
  65.6 0.0 copy-done.2
  65.6 0.1 copy.21
  65.7 0.0 copy-done.3
  65.7 0.1 iota_compare_fusion.3
  65.8 4.5 %fusion = bf16[128,8,3,128]{3,2,1,0:T(4,128)(2,1)S(1)} fusion(f32[8,6,128,128]{2,1,0,3:T(8,128)} %copy.25, s32[128,3]{1,0:T(8,128)S(1)} %copy.21, pred[128,3]{1,0:T(8,128)(4,1)S(1)} %iota_compare_fusion.3), kind=kOutput, calls=%fused_computation.3 | convolution fusion | flops 28709376 | bytes 3934080 | tf_op jit(solution)/shard_map/pbni,ikb->ipkn/dot_general | solution.py:30
  70.3 0.7 convert_element_type.29
  71.0 0.7 gather_fusion
  71.7 0.2 broadcast_select_fusion
  72.0 22.3 %all_to_all.18 = bf16[128,8,384]{2,1,0:T(8,128)(2,1)S(1)} all-to-all(bf16[128,8,384]{2,1,0:T(8,128)(2,1)S(1)} %broadcast_select_fusion), channel_id=1, replica_groups=mesh['aux'=8,'lmo'=4] {'aux','lmo'}, dimensions={0} | all-to-all | bytes 1572864 | tf_op jit(solution)/shard_map/all_to_all | solution.py:46
  94.3 0.0 copy-done
  94.3 0.4 convolution_convert_fusion.1
  94.7 0.0 copy-start.1
  94.7 1.3 %convolution_multiply_fusion = f32[4,256,256]{2,1,0:T(8,128)} fusion(bf16[4,256,256]{2,1,0:T(8,128)(2,1)S(1)} %convolution_convert_fusion.1), kind=kOutput, calls=%fused_computation.4 | convolution fusion | flops 134479872 | bytes 1572864 | tf_op jit(solution)/shard_map/rpa,rpb->rab/dot_general | solution.py:52
  96.0 0.0 copy-done.1
  (2 shorter events, 0.0 us)
Async XLA Ops:
  0.6 93.6 %copy-start = (bf16[4,384,256]{2,1,0:T(8,128)(2,1)S(1)}, bf16[4,384,256]{2,1,0:T(8,128)(2,1)}, u32[]{:S(2)}) copy-start(bf16[4,384,256]{2,1,0:T(8,128)(2,1)} %param.15) | copy-start | bytes 2359300
  60.6 5.0 %copy-start.2 = (s32[128,3]{0,1:T(4,128)S(1)}, s32[128,3]{0,1:T(4,128)}, u32[]{:S(2)}) copy-start(s32[128,3]{0,1:T(4,128)} %param.12) | copy-start | bytes 4612
  60.6 5.1 %copy-start.3 = (s32[128]{0:T(128)S(1)}, s32[128]{0:T(128)}, u32[]{:S(2)}) copy-start(s32[128]{0:T(128)} %param.13) | copy-start | bytes 1540
  94.7 1.3 %copy-start.1 = (bf16[4,256,256]{2,1,0:T(8,128)(2,1)}, bf16[4,256,256]{2,1,0:T(8,128)(2,1)S(1)}, u32[]{:S(2)}) copy-start(bf16[4,256,256]{2,1,0:T(8,128)(2,1)S(1)} %convolution_convert_fusion.1) | copy-start | bytes 1572868
where the time goes:
time: 96.4 us; the launch traced here: 96 us
  blocking collectives  66 us (68%)
  matrix products  15.6 us (16%)
  local copies, waits for them, and re-layouts  11.2 us (12%)
  other arithmetic  2.43 us (3%)
    all_gather x1, blocking collectives, shards(): all_coef = lax.all_gather(lmo_coef, ('aux', 'lmo'), axis=0, tiled=True)  43.7 us
    all_to_all x1, blocking collectives, shards(): lax.all_to_all(ordered, ('aux', 'lmo'), split_axis=0, concat_axis=1, tile...  22.3 us
    dot_general x1, matrix products, shards(): jnp.dot(aux_ints.reshape(row_total * ao_total, ao_total), dense_coef, pre...  8.53 us
    another operation x1, local copies, waits for them, and re-layouts, select(): tiled = half_ints.reshape(row_total, blocks, BLK, lmo_total)  5.03 us
    dot_general x1, matrix products, select(): jnp.einsum('pbni,ikb->ipkn', tiled, onehot, precision=lax.Precision.HIGHEST)  4.46 us
    dot_general x1, local copies, waits for them, and re-layouts, shards(): jnp.dot(aux_ints.reshape(row_total * ao_total, ao_total), dense_coef, pre...  3.55 us

commit v1 on v0

v1 whole, which is shorter than its diff:
```python
import functools

import jax
import jax.numpy as jnp
from jax import lax
from jax.experimental import pallas as pl
from jax.experimental.pallas import tpu as pltpu
from jax.sharding import PartitionSpec as P

BLK = 128
DB = 3
PB = 3
USED = 8
MESH = pl.DeviceIdType.MESH


def exchange(
    n_aux, n_lmo,
    aux_hbm, lmo_ref, ao_dom, ao_cnt, pao_dom, pao_cnt, order, recv,
    aux, coef_all, coef32, dense, half, tab, send,
    aux_sem, coef_send, coef_recv, out_send, out_recv, own_sem,
):
    dev = n_aux * n_lmo
    rows, ao, _ = aux_hbm.shape
    blocks = ao // BLK
    per = lmo_ref.shape[0]
    lmos = per * dev
    me = lax.axis_index("aux") * n_lmo + lax.axis_index("lmo")

    def coords(d):
        return (d // n_lmo, lax.rem(d, n_lmo))

    def partner(t):
        return lax.rem(me + t, dev)

    def load(p):
        return pltpu.make_async_copy(aux_hbm.at[p], aux.at[p], aux_sem.at[p])

    for p in range(rows):
        load(p).start()

    barrier = pltpu.get_barrier_semaphore()

    @pl.loop(1, dev)
    def _(t):
        pl.semaphore_signal(barrier, inc=1, device_id=coords(partner(t)), device_id_type=MESH)

    pl.semaphore_wait(barrier, dev - 1)

    def coef_copy(slot, d):
        return pltpu.make_async_remote_copy(
            src_ref=lmo_ref, dst_ref=coef_all.at[slot],
            send_sem=coef_send.at[d], recv_sem=coef_recv.at[slot],
            device_id=coords(d), device_id_type=MESH,
        )

    @pl.loop(1, dev)
    def _(t):
        coef_copy(me, partner(t)).start()

    coef_all[me] = lmo_ref[...]

    @pl.loop(0, dev)
    def _(d):
        lmo = [order[d * per + j] for j in range(per)]
        cnt = [pao_cnt[i] for i in lmo]
        for s in range(USED):
            i, k = lmo[0], jnp.int32(s)
            start = jnp.int32(0)
            for j in range(1, per):
                start = start + cnt[j - 1]
                past = s >= start
                i = jnp.where(past, lmo[j], i)
                k = jnp.where(past, s - start, k)
            tab[d * USED + s] = i * blocks + pao_dom[jnp.minimum(k, PB - 1), i]

    @pl.loop(1, dev)
    def _(t):
        d = partner(t)
        coef_copy(d, d).wait_recv()

    for d in range(dev):
        coef32[d * per:(d + 1) * per, :] = coef_all[d].astype(jnp.float32)

    eye = lax.broadcasted_iota(jnp.int32, (lmos, lmos), 0) == lax.broadcasted_iota(
        jnp.int32, (lmos, lmos), 1
    )
    where_to = []
    for k in range(DB):
        block = jnp.where(ao_cnt[...] > k, ao_dom[k:k + 1, :], -1).astype(jnp.float32)
        column = jnp.sum(jnp.where(eye, block, 0.0), axis=1, keepdims=True)
        where_to.append(jnp.broadcast_to(column, (lmos, BLK)))
    for b in range(blocks):
        total = jnp.zeros((lmos, BLK), jnp.float32)
        for k in range(DB):
            total = jnp.where(where_to[k] == b, coef32[:, k * BLK:(k + 1) * BLK], total)
        dense[:, b * BLK:(b + 1) * BLK] = total.astype(jnp.bfloat16)

    wide = 2 * BLK
    flat = half.reshape(lmos * blocks * rows, BLK)
    for p in range(rows):
        load(p).wait()
        for c in range(ao // wide):
            out = lax.dot_general(
                dense[...], aux[p, c * wide:(c + 1) * wide, :],
                (((1,), (1,)), ((), ())), preferred_element_type=jnp.float32,
            )
            for h in range(2):
                b = c * 2 + h
                flat[pl.ds(b * rows + p, lmos, stride=blocks * rows), :] = (
                    out[:, h * BLK:(h + 1) * BLK]
                )

    def pack(d):
        for s in range(USED):
            row = tab[d * USED + s]
            send[d, s] = half[row].astype(jnp.bfloat16)

    def out_copy(slot, d):
        return pltpu.make_async_remote_copy(
            src_ref=send.at[d], dst_ref=recv.at[slot],
            send_sem=out_send.at[d], recv_sem=out_recv.at[slot],
            device_id=coords(d), device_id_type=MESH,
        )

    pack(partner(1))

    @pl.loop(1, dev)
    def _(t):
        pack(partner(t + 1))
        out_copy(me, partner(t)).start()

    own = pltpu.make_async_copy(send.at[me], recv.at[me], own_sem)
    own.start()

    @pl.loop(1, dev)
    def _(t):
        d = partner(t)
        coef_copy(d, d).wait_send()
        out_copy(d, d).wait_send()
        out_copy(d, d).wait_recv()

    own.wait()


def contract(n_lmo, per, recv, coef, pao_cnt, order, pair, metric, kept):
    g = pl.program_id(0)
    me = lax.axis_index("aux") * n_lmo + lax.axis_index("lmo")
    dev, _, rows, _ = recv.shape
    start = jnp.int32(0)
    for j in range(per - 1):
        start = start + jnp.where(j < g, pao_cnt[order[me * per + j]], 0)
    count = pao_cnt[order[me * per + g]]
    for k in range(PB):
        slot = jnp.minimum(start + k, USED - 1)
        tile = recv[:, slot].astype(jnp.float32).reshape(dev * rows, BLK)
        tile = jnp.where(k < count, tile, 0.0)
        kept[:, k * BLK:(k + 1) * BLK] = tile.astype(jnp.bfloat16)
    row = jnp.dot(kept[...], coef[0], preferred_element_type=jnp.float32).astype(jnp.bfloat16)
    pair[0] = row
    metric[0] = lax.dot_general(
        row, row, (((0,), (0,)), ((), ())), preferred_element_type=jnp.float32
    ) / (dev * rows)


def shards(mesh, aux_ints, lmo_coef, ao_domain, ao_count, pao_domain, pao_count, owner_order, pao_coef):
    n_aux, n_lmo = mesh.shape["aux"], mesh.shape["lmo"]
    dev = n_aux * n_lmo
    rows, ao, _ = aux_ints.shape
    blocks = ao // BLK
    per = lmo_coef.shape[0]
    lmos = per * dev
    npao = pao_coef.shape[2]
    vmem = pl.BlockSpec(memory_space=pltpu.VMEM)
    smem = pl.BlockSpec(memory_space=pltpu.SMEM)
    anywhere = pl.BlockSpec(memory_space=pl.ANY)
    recv = pl.pallas_call(
        functools.partial(exchange, n_aux, n_lmo),
        out_shape=jax.ShapeDtypeStruct((dev, USED, rows, BLK), jnp.bfloat16),
        in_specs=[anywhere, vmem, vmem, vmem, smem, smem, smem],
        out_specs=anywhere,
        scratch_shapes=[
            pltpu.VMEM((rows, ao, ao), jnp.bfloat16),
            pltpu.VMEM((dev, per, DB * BLK), jnp.bfloat16),
            pltpu.VMEM((lmos, DB * BLK), jnp.float32),
            pltpu.VMEM((lmos, ao), jnp.bfloat16),
            pltpu.VMEM((lmos * blocks, rows, BLK), jnp.float32),
            pltpu.SMEM((dev * USED,), jnp.int32),
            pltpu.VMEM((dev, USED, rows, BLK), jnp.bfloat16),
            pltpu.SemaphoreType.DMA((rows,)),
            pltpu.SemaphoreType.DMA((dev,)),
            pltpu.SemaphoreType.DMA((dev,)),
            pltpu.SemaphoreType.DMA((dev,)),
            pltpu.SemaphoreType.DMA((dev,)),
            pltpu.SemaphoreType.DMA,
        ],
        compiler_params=pltpu.CompilerParams(
            collective_id=0, has_side_effects=True, vmem_limit_bytes=60 * 2**20
        ),
        name="exchange",
    )(aux_ints, lmo_coef, ao_domain.T, ao_count.reshape(1, lmos), pao_domain.T, pao_count, owner_order)
    pair, metric = pl.pallas_call(
        functools.partial(contract, n_lmo, per),
        grid=(per,),
        out_shape=(
            jax.ShapeDtypeStruct((per, dev * rows, npao), jnp.bfloat16),
            jax.ShapeDtypeStruct((per, npao, npao), jnp.float32),
        ),
        in_specs=[
            pl.BlockSpec((dev, USED, rows, BLK), lambda g: (0, 0, 0, 0)),
            pl.BlockSpec((1, PB * BLK, npao), lambda g: (g, 0, 0)),
            smem,
            smem,
        ],
        out_specs=(
            pl.BlockSpec((1, dev * rows, npao), lambda g: (g, 0, 0)),
            pl.BlockSpec((1, npao, npao), lambda g: (g, 0, 0)),
        ),
        scratch_shapes=[pltpu.VMEM((dev * rows, PB * BLK), jnp.bfloat16)],
        name="contract",
    )(recv, pao_coef, pao_count, owner_order)
    return pair, metric


def solution(mesh):
    split = ("aux", "lmo")
    placed = (P(split, None, None), P(split, None), P(), P(), P(), P(), P(), P(split, None, None))
    return jax.shard_map(
        functools.partial(shards, mesh),
        mesh=mesh,
        in_specs=placed,
        out_specs=(P(split, None, None), P(split, None, None)),
        check_vma=False,
    )
```

time: 96.4 us -> 36.2 us (0.38)
  the two profiles are of different devices: /device:TPU:0 before, /device:TPU:11 now
where the time goes in v1:
time: 36.2 us; the launch traced here: 36 us
  Pallas kernels  35.4 us (98%)
  between operations  0.64 us (2%)
    pallas_call x1, Pallas kernels, shards(): pl.pallas_call(functools.partial(exchange, n_aux, n_lmo), out_shape=jax.S...  30.9 us
    pallas_call x1, Pallas kernels, shards(): pl.pallas_call(functools.partial(contract, n_lmo, per), grid=(per,), out_...  4.54 us

profile of v1, /device:TPU:11, one launch (start us, length us, event | category | flops | bytes accessed | tf_op | source)
XLA Modules:
  0.0 36.0 jit_solution(16299150397050365491)
XLA Ops:
  0.6 30.9 %exchange.1.recv = bf16[32,8,8,128]{3,2,1,0:T(8,128)(2,1)} custom-call(bf16[8,768,768]{2,1,0:T(8,128)(2,1)} %aux_hbm.1, bf16[4,384]{1,0:T(4,128)(2,1)} %lmo_ref.1, s32[3,128]{1,0:T(4,128)} %bitcast.3, s32[1,128]{1,0:T(1,128)} %bitcast.5, s32[3,128]{1,0:T(4,128)} %bitcast.4, s32[128]{0:T(128)} %pao_cnt.3, s32[128]{0:T(128)} %order.3), custom_call_target="tpu_custom_call" | custom-call | tf_op jit(solution)/shard_map/exchange/pallas_call | solution.py:177
  31.5 4.5 %contract.1 = (bf16[4,256,256]{2,1,0:T(8,128)(2,1)}, f32[4,256,256]{2,1,0:T(8,128)}) custom-call(bf16[32,8,8,128]{3,2,1,0:T(8,128)(2,1)} %exchange.1.recv, bf16[4,384,256]{2,1,0:T(8,128)(2,1)} %coef.1, s32[128]{0:T(128)} %pao_cnt.3, s32[128]{0:T(128)} %order.3), custom_call_target="tpu_custom_call" | custom-call | tf_op jit(solution)/shard_map/contract/pallas_call | solution.py:202

commit v2 on v1

--- a/solution.py
+++ b/solution.py
@@ -10,6 +10,7 @@
 BLK = 128
 DB = 3
 PB = 3
+PARTS = 1
 USED = 8
 MESH = pl.DeviceIdType.MESH
 
@@ -96,71 +97,89 @@
             total = jnp.where(where_to[k] == b, coef32[:, k * BLK:(k + 1) * BLK], total)
         dense[:, b * BLK:(b + 1) * BLK] = total.astype(jnp.bfloat16)
 
-    wide = 2 * BLK
     flat = half.reshape(lmos * blocks * rows, BLK)
-    for p in range(rows):
-        load(p).wait()
-        for c in range(ao // wide):
-            out = lax.dot_general(
-                dense[...], aux[p, c * wide:(c + 1) * wide, :],
-                (((1,), (1,)), ((), ())), preferred_element_type=jnp.float32,
-            )
-            for h in range(2):
-                b = c * 2 + h
-                flat[pl.ds(b * rows + p, lmos, stride=blocks * rows), :] = (
-                    out[:, h * BLK:(h + 1) * BLK]
+    chunk = rows // PARTS
+
+    def transform(g):
+        for p in range(g * chunk, (g + 1) * chunk):
+            load(p).wait()
+        out = lax.dot_general(
+            dense[...], aux[g * chunk:(g + 1) * chunk].reshape(chunk * ao, ao),
+            (((1,), (1,)), ((), ())), preferred_element_type=jnp.float32,
+        )
+        for q in range(chunk):
+            for b in range(blocks):
+                first = q * ao + b * BLK
+                flat[pl.ds(b * rows + g * chunk + q, lmos, stride=blocks * rows), :] = (
+                    out[:, first:first + BLK]
                 )
 
-    def pack(d):
+    def pack(g, d):
         for s in range(USED):
             row = tab[d * USED + s]
-            send[d, s] = half[row].astype(jnp.bfloat16)
-
-    def out_copy(slot, d):
+            send[g, d, s] = half[row, g * chunk:(g + 1) * chunk, :].astype(jnp.bfloat16)
+
+    def out_copy(g, slot, d):
         return pltpu.make_async_remote_copy(
-            src_ref=send.at[d], dst_ref=recv.at[slot],
-            send_sem=out_send.at[d], recv_sem=out_recv.at[slot],
+            src_ref=send.at[g, d], dst_ref=recv.at[g, slot],
+            send_sem=out_send.at[g, d], recv_sem=out_recv.at[g, slot],
             device_id=coords(d), device_id_type=MESH,
         )
 
-    pack(partner(1))
-
-    @pl.loop(1, dev)
-    def _(t):
-        pack(partner(t + 1))
-        out_copy(me, partner(t)).start()
-
-    own = pltpu.make_async_copy(send.at[me], recv.at[me], own_sem)
-    own.start()
+    def own_copy(g):
+        return pltpu.make_async_copy(send.at[g, me], recv.at[g, me], own_sem.at[g])
+
+    for g in range(PARTS):
+        transform(g)
+        pack(g, partner(1))
+
+        @pl.loop(1, dev)
+        def _(t):
+            pack(g, partner(t + 1))
+            out_copy(g, me, partner(t)).start()
+
+        own_copy(g).start()
 
     @pl.loop(1, dev)
     def _(t):
         d = partner(t)
         coef_copy(d, d).wait_send()
-        out_copy(d, d).wait_send()
-        out_copy(d, d).wait_recv()
-
-    own.wait()
-
-
-def contract(n_lmo, per, recv, coef, pao_cnt, order, pair, metric, kept):
-    g = pl.program_id(0)
+        for g in range(PARTS):
+            out_copy(g, d, d).wait_send()
+            out_copy(g, d, d).wait_recv()
+
+    for g in range(PARTS):
+        own_copy(g).wait()
+
+
+def contract(n_lmo, per, recv, coef, pao_cnt, order, pair, metric, pair_out, metric_out, sem):
     me = lax.axis_index("aux") * n_lmo + lax.axis_index("lmo")
-    dev, _, rows, _ = recv.shape
+    _, dev, _, chunk, _ = recv.shape
+    rows = PARTS * chunk
     start = jnp.int32(0)
-    for j in range(per - 1):
-        start = start + jnp.where(j < g, pao_cnt[order[me * per + j]], 0)
-    count = pao_cnt[order[me * per + g]]
-    for k in range(PB):
-        slot = jnp.minimum(start + k, USED - 1)
-        tile = recv[:, slot].astype(jnp.float32).reshape(dev * rows, BLK)
-        tile = jnp.where(k < count, tile, 0.0)
-        kept[:, k * BLK:(k + 1) * BLK] = tile.astype(jnp.bfloat16)
-    row = jnp.dot(kept[...], coef[0], preferred_element_type=jnp.float32).astype(jnp.bfloat16)
-    pair[0] = row
-    metric[0] = lax.dot_general(
-        row, row, (((0,), (0,)), ((), ())), preferred_element_type=jnp.float32
-    ) / (dev * rows)
+    copies = []
+    for g in range(per):
+        count = pao_cnt[order[me * per + g]]
+        tiles = []
+        for k in range(PB):
+            slot = jnp.minimum(start + k, USED - 1)
+            tile = jnp.concatenate(
+                [recv[h, :, slot].astype(jnp.float32) for h in range(PARTS)], axis=1
+            ).reshape(dev * rows, BLK)
+            tiles.append(jnp.where(k < count, tile, 0.0).astype(jnp.bfloat16))
+        start = start + count
+        row = jnp.dot(
+            jnp.concatenate(tiles, axis=1), coef[g], preferred_element_type=jnp.float32
+        ).astype(jnp.bfloat16)
+        pair_out[g] = row
+        metric_out[g] = lax.dot_general(
+            row, row, (((0,), (0,)), ((), ())), preferred_element_type=jnp.float32
+        ) / (dev * rows)
+        for c, (src, dst) in enumerate(((pair_out, pair), (metric_out, metric))):
+            copies.append(pltpu.make_async_copy(src.at[g], dst.at[g], sem.at[g, c]))
+            copies[-1].start()
+    for copy in copies:
+        copy.wait()
 
 
 def shards(mesh, aux_ints, lmo_coef, ao_domain, ao_count, pao_domain, pao_count, owner_order, pao_coef):
@@ -176,7 +195,7 @@
     anywhere = pl.BlockSpec(memory_space=pl.ANY)
     recv = pl.pallas_call(
         functools.partial(exchange, n_aux, n_lmo),
-        out_shape=jax.ShapeDtypeStruct((dev, USED, rows, BLK), jnp.bfloat16),
+        out_shape=jax.ShapeDtypeStruct((PARTS, dev, USED, rows // PARTS, BLK), jnp.bfloat16),
         in_specs=[anywhere, vmem, vmem, vmem, smem, smem, smem],
         out_specs=anywhere,
         scratch_shapes=[
@@ -186,13 +205,13 @@
             pltpu.VMEM((lmos, ao), jnp.bfloat16),
             pltpu.VMEM((lmos * blocks, rows, BLK), jnp.float32),
             pltpu.SMEM((dev * USED,), jnp.int32),
-            pltpu.VMEM((dev, USED, rows, BLK), jnp.bfloat16),
+            pltpu.VMEM((PARTS, dev, USED, rows // PARTS, BLK), jnp.bfloat16),
             pltpu.SemaphoreType.DMA((rows,)),
             pltpu.SemaphoreType.DMA((dev,)),
             pltpu.SemaphoreType.DMA((dev,)),
-            pltpu.SemaphoreType.DMA((dev,)),
-            pltpu.SemaphoreType.DMA((dev,)),
-            pltpu.SemaphoreType.DMA,
+            pltpu.SemaphoreType.DMA((PARTS, dev)),
+            pltpu.SemaphoreType.DMA((PARTS, dev)),
+            pltpu.SemaphoreType.DMA((PARTS,)),
         ],
         compiler_params=pltpu.CompilerParams(
             collective_id=0, has_side_effects=True, vmem_limit_bytes=60 * 2**20
@@ -201,22 +220,22 @@
     )(aux_ints, lmo_coef, ao_domain.T, ao_count.reshape(1, lmos), pao_domain.T, pao_count, owner_order)
     pair, metric = pl.pallas_call(
         functools.partial(contract, n_lmo, per),
-        grid=(per,),
         out_shape=(
             jax.ShapeDtypeStruct((per, dev * rows, npao), jnp.bfloat16),
             jax.ShapeDtypeStruct((per, npao, npao), jnp.float32),
         ),
         in_specs=[
-            pl.BlockSpec((dev, USED, rows, BLK), lambda g: (0, 0, 0, 0)),
-            pl.BlockSpec((1, PB * BLK, npao), lambda g: (g, 0, 0)),
+            vmem,
+            vmem,
             smem,
             smem,
         ],
-        out_specs=(
-            pl.BlockSpec((1, dev * rows, npao), lambda g: (g, 0, 0)),
-            pl.BlockSpec((1, npao, npao), lambda g: (g, 0, 0)),
-        ),
-        scratch_shapes=[pltpu.VMEM((dev * rows, PB * BLK), jnp.bfloat16)],
+        out_specs=(anywhere, anywhere),
+        scratch_shapes=[
+            pltpu.VMEM((per, dev * rows, npao), jnp.bfloat16),
+            pltpu.VMEM((per, npao, npao), jnp.float32),
+            pltpu.SemaphoreType.DMA((per, 2)),
+        ],
         name="contract",
     )(recv, pao_coef, pao_count, owner_order)
     return pair, metric

time: 36.2 us -> 34 us (0.939)
  Pallas kernels: 35.4 us -> 33.2 us
    pallas_call x1, Pallas kernels: 30.9 us -> 29.5 us  [shards(): pl.pallas_call(functools.partial(exchange, n_aux, n_lmo), out_shape=jax.S...]
    pallas_call x1, Pallas kernels: 4.54 us -> 3.66 us  [shards(): pl.pallas_call(functools.partial(contract, n_lmo, per), out_shape=(jax.Sh...]
where the time goes in v2:
time: 34 us; the launch traced here: 33.8 us
  Pallas kernels  33.2 us (98%)
  between operations  0.64 us (2%)
    pallas_call x1, Pallas kernels, shards(): pl.pallas_call(functools.partial(exchange, n_aux, n_lmo), out_shape=jax.S...  29.5 us
    pallas_call x1, Pallas kernels, shards(): pl.pallas_call(functools.partial(contract, n_lmo, per), out_shape=(jax.Sh...  3.66 us

profile of v2, /device:TPU:11, one launch (start us, length us, event | category | flops | bytes accessed | tf_op | source)
XLA Modules:
  0.0 33.8 jit_solution(6275170331936301732)
XLA Ops:
  0.6 29.5 %exchange.1.recv = bf16[1,32,8,8,128]{4,3,2,1,0:T(8,128)(2,1)} custom-call(bf16[8,768,768]{2,1,0:T(8,128)(2,1)} %aux_hbm.1, bf16[4,384]{1,0:T(4,128)(2,1)} %lmo_ref.1, s32[3,128]{1,0:T(4,128)} %bitcast.3, s32[1,128]{1,0:T(1,128)} %bitcast.5, s32[3,128]{1,0:T(4,128)} %bitcast.4, s32[128]{0:T(128)} %pao_cnt.3, s32[128]{0:T(128)} %order.3), custom_call_target="tpu_custom_call" | custom-call | tf_op jit(solution)/shard_map/exchange/pallas_call | solution.py:196
  30.2 3.7 %contract.1 = (bf16[4,256,256]{2,1,0:T(8,128)(2,1)}, f32[4,256,256]{2,1,0:T(8,128)}) custom-call(bf16[1,32,8,8,128]{4,3,2,1,0:T(8,128)(2,1)} %exchange.1.recv, bf16[4,384,256]{2,1,0:T(8,128)(2,1)} %coef.1, s32[128]{0:T(128)} %pao_cnt.3, s32[128]{0:T(128)} %order.3), custom_call_target="tpu_custom_call" | custom-call | tf_op jit(solution)/shard_map/contract/pallas_call | solution.py:221
